TPU v7x, 32 devices: a whole 2x2x4 slice. The times are simulated.
32 devices in a mesh: expert: 4 (over y, x), rep: 4 (over z), hid: 2 (over core).
Axes of the slice: x: 2, y: 2, z: 4, core: 2. Of those that a mesh axis runs over, the one named last changes fastest.
Arguments:
- calib_rows: bfloat16 [8192, 6144], P(('expert', 'rep'), 'hid'), may hold values from -6 to 6
- routes: int32 [8192, 2], P(('expert', 'rep')), may hold values from 0 to 7, all different within a row; in each aligned block of 512 rows (0 to 511, 512 to 1023, ...) at most 256 rows name the same one
- sketch_seed: int32 [6144, 512], P('hid'), may hold values from -1 to 1
- up_weight: bfloat16 [8, 6144, 16384], P('expert', 'hid', 'rep'), may hold values from -0.078125 to 0.078125
Outputs:
- projected: float32 [16384, 8, 512], P(('rep', 'hid'), 'expert')
Inputs may be any that keep to these rules, and one draw needn't show every extreme that they name: `routes`: each row names 2 different experts. In each aligned block of 512 rows no expert is named by more than 256 rows, and every expert is named somewhere.
All inputs are finite; a program needn't handle non-finite values.
Results may differ from a plain program's by a relative error of at most 0.0037.
Values may be sent and summed in bfloat16 or wider, within the bound.
No kernel may reach another device: no remote copies, remote signals or barrier semaphores. Data moves between devices by JAX's collectives and lax.ppermute only.
A program may use at most 192 MiB of HBM per device.

v0:
```python
import jax
import jax.numpy as jnp
from jax import lax
from jax.sharding import PartitionSpec as P

D = 6144
EXPERTS = 8
CAP = 256
damping = 0.25


def shards(calib_rows, routes, sketch_seed, up_weight):
    exp_local = up_weight.shape[0]
    signs_half = sketch_seed.astype(jnp.bfloat16)
    signs_full = sketch_seed.astype(jnp.float32)
    expert_ids = jnp.arange(EXPERTS, dtype=jnp.int32)
    member = jnp.sum((routes[:, :, None] == expert_ids[None, None, :]).astype(jnp.float32), axis=1)
    row_squares = jnp.sum(jnp.square(calib_rows.astype(jnp.float32)), axis=1)
    leader = (lax.axis_index("hid") == 0).astype(jnp.float32)
    counts, squares = lax.psum(
        (jnp.sum(member, axis=0) * leader, jnp.sum(member * row_squares[:, None], axis=0)),
        ("expert", "rep", "hid"),
    )
    flat_routes = routes.reshape(-1)
    one_hot = (flat_routes[:, None] == expert_ids[None, :]).astype(jnp.int32)
    before = jnp.cumsum(one_hot, axis=0) - one_hot
    slot_index = jnp.sum(before * one_hot, axis=1)
    repeated = jnp.repeat(calib_rows, routes.shape[1], axis=0)
    outgoing = jnp.zeros((EXPERTS, CAP, calib_rows.shape[1]), jnp.bfloat16)
    outgoing = outgoing.at[flat_routes, slot_index].set(repeated)
    outgoing = outgoing.reshape(lax.axis_size("expert"), exp_local, CAP, calib_rows.shape[1])
    rows_here = lax.all_to_all(outgoing, "expert", split_axis=0, concat_axis=2, tiled=True)[0]
    partial_value = jnp.einsum(
        "kmd,dr->kmr", rows_here, signs_half, preferred_element_type=jnp.float32
    )
    summed_rows = lax.psum(partial_value, "hid")
    masked = summed_rows.astype(jnp.bfloat16)
    partial_gram = jnp.einsum("kmd,kmr->kdr", rows_here, masked, preferred_element_type=jnp.float32)
    summed = lax.psum(partial_gram, "rep")
    first_expert = lax.axis_index("expert") * exp_local
    row_counts = lax.dynamic_slice_in_dim(counts, first_expert, exp_local)
    square_sums = lax.dynamic_slice_in_dim(squares, first_expert, exp_local)
    ridge = damping * square_sums / (row_counts * D)
    sketch = (
        summed / row_counts[:, None, None] + ridge[:, None, None] * signs_full[None, :, :]
    ).astype(jnp.bfloat16)
    return lax.psum_scatter(
        jnp.einsum("edf,edr->fer", up_weight, sketch, preferred_element_type=jnp.float32),
        "hid",
        scatter_dimension=0,
        tiled=True,
    )


def solution(mesh):
    in_specs = (
        P(("expert", "rep"), "hid"),
        P(("expert", "rep"), None),
        P("hid", None),
        P("expert", "hid", "rep"),
    )
    out_specs = P(("rep", "hid"), "expert", None)
    return jax.shard_map(shards, mesh=mesh, in_specs=in_specs, out_specs=out_specs, check_vma=False)
```

profile of v0, /device:TPU:0, one launch (start us, length us, event | category | flops | bytes accessed | tf_op | source)
XLA Modules:
  0.0 748.2 jit_solution(2252918654287226031)
XLA Ops:
  6.5 0.8 copy.22
  7.7 0.2 reshape.73
  7.9 2.3 reduce-window.6
  10.2 0.3 slice_reduce_fusion
  10.7 0.8 and_reduce_fusion
  11.5 0.7 multiply_reduce_fusion.2
  12.2 7.0 broadcast_in_dim.5
  19.3 13.6 %reshape.84 = bf16[1024,3072]{1,0:T(8,128)(2,1)} reshape(bf16[512,2,3072]{2,1,0:T(2,128)(2,1)} %broadcast_in_dim.5) | data formatting | bytes 12582912 | tf_op jit(solution)/shard_map/reshape | solution.py:28
  32.9 17.2 %scatter_custom_fusion = bf16[2048,3072]{1,0:T(8,128)(2,1)} fusion(s32[1024]{0:T(1024)S(1)} %broadcast_select_fusion, bf16[1024,3072]{1,0:T(8,128)(2,1)} %reshape.84, bf16[]{:T(256)} %constant.10.clone.1), kind=kCustom, calls=%fused_computation.3 | custom fusion | bytes 12583424
  50.0 144.0 %all_to_all.15 = bf16[4,2,256,3072]{3,2,1,0:T(8,128)(2,1)S(1)} all-to-all(bf16[4,2,256,3072]{3,2,1,0:T(8,128)(2,1)} %bitcast.35), channel_id=1, replica_groups=mesh['expert'=4,'rep'=4,'hid'=2] {'expert'}, dimensions={0} | all-to-all | bytes 25165824 | tf_op jit(solution)/shard_map/all_to_all | solution.py:32
  194.0 2.3 copy.25
  196.3 4.5 copy-done
  200.8 8.8 %fusion.5 = f32[2,1024,512]{2,1,0:T(8,128)} fusion(bf16[2,1024,3072]{2,1,0:T(8,128)(2,1)S(1)} %bitcast.37, s32[3072,512]{1,0:T(8,128)S(1)} %bitcast.40), kind=kOutput, calls=%fused_computation.9 | convolution fusion | flops 6444023808 | bytes 23068672 | tf_op jit(solution)/shard_map/kmd,dr->kmr/dot_general | solution.py:33
  209.6 14.9 %all-reduce.5 = bf16[2,1024,512]{2,1,0:T(8,128)(2,1)S(1)} all-reduce(f32[2,1024,512]{2,1,0:T(8,128)} %fusion.5), channel_id=1, replica_groups=mesh['expert'=4,'rep'=4,'hid'=2] {'hid'}, use_global_device_ids=true, to_apply=%region_4.0 | all-reduce | flops 1048576 | bytes 6291456 | tf_op jit(solution)/shard_map/psum | solution.py:36
  224.5 12.4 %fusion.14 = f32[2,3072,512]{2,1,0:T(8,128)} fusion(bf16[2,1024,3072]{2,1,0:T(8,128)(2,1)} %bitcast.38, bf16[2,1024,512]{2,1,0:T(8,128)(2,1)S(1)} %all-reduce.5), kind=kOutput, calls=%fused_computation.35 | convolution fusion | flops 6442450944 | bytes 27262976 | tf_op jit(solution)/shard_map/kmd,kmr->kdr/dot_general | solution.py:38
  237.0 0.6 copy-done.2
  237.7 1.1 copy-done.1
  238.8 0.7 multiply_reduce_fusion
  239.6 44.5 %all-reduce = (f32[8]{0:T(128)S(1)}, f32[8]{0:T(128)S(1)}) all-reduce(f32[8]{0:T(128)S(1)} %broadcast_multiply_fusion, f32[8]{0:T(128)S(1)} %multiply_reduce_fusion.1), channel_id=1, replica_groups=mesh['expert'=4,'rep'=4,'hid'=2] {'expert','rep','hid'}, use_global_device_ids=true, to_apply=%region_7.8 | all-reduce | flops 16 | bytes 128 | tf_op jit(solution)/shard_map/psum | solution.py:20
  284.1 6.3 convert_element_type.35
  290.4 373.7 %all-reduce.4.cloned.1.call-done = f32[2,3072,512]{2,1,0:T(8,128)} async-done(((f32[2,3072,512]{2,1,0:T(8,128)}), f32[2,3072,512]{2,1,0:T(8,128)}) %all-reduce.4.cloned.1.call-update) | async-done | bytes 12582928 | tf_op jit(solution)/shard_map/psum | solution.py:39
  664.2 40.0 %convolution_bitcast_fusion = f32[4096,2,512]{0,2,1:T(8,128)} fusion(bf16[2,3072,4096]{2,1,0:T(8,128)(2,1)} %param.7, f32[2,3072,512]{2,1,0:T(8,128)} %all-reduce.4.cloned.1.call-done, f32[3072,512]{1,0:T(8,128)} %convert_element_type.35, f32[2]{0:T(128)S(1)} %get-tuple-element.9, f32[2]{0:T(128)S(1)} %get-tuple-element.10), kind=kOutput, calls=%fused_computation.2 | convolution fusion | flops 25782386688 | bytes 85983248 | tf_op jit(solution)/shard_map/edf,edr->fer/dot_general | solution.py:48
  704.2 24.0 %reduce-scatter.2.cloned.1.call-done = f32[2048,2,512]{0,2,1:T(8,128)} async-done(((f32[4096,2,512]{0,2,1:T(8,128)}), f32[2048,2,512]{0,2,1:T(8,128)}) %reduce-scatter.2.cloned.1.call-update) | async-done | bytes 8388624 | tf_op jit(solution)/shard_map/reduce_scatter | solution.py:47
  728.2 13.1 %copy.28 = f32[2048,2,512]{2,1,0:T(2,128)} copy(f32[2048,2,512]{0,2,1:T(8,128)} %reduce-scatter.2.cloned.1.call-done) | data formatting | bytes 16777216 | tf_op jit(solution)/shard_map/reduce_scatter | solution.py:47
  (24 shorter events, 1.0 us)
Async XLA Ops:
  6.5 657.6 %all-reduce.4.cloned.1.call-start = ((), (), s32[]{:S(2)}) async-start(), calls=%async_computation.2 | async-start | bytes 25165824 | tf_op jit(solution)/shard_map/psum | solution.py:39
  50.0 150.7 %slice-start = ((s8[6291456]{0:T(1024)(128)(4,1)}), s8[4194304]{0:T(1024)(128)(4,1)S(1)}, s32[]{:S(2)}) async-start(s8[6291456]{0:T(1024)(128)(4,1)} %bitcast.39), calls=%async_computation.4 | async-start | bytes 8388608
  194.0 6.8 slice-start.1
  196.3 4.5 copy-start
  236.9 0.7 copy-start.2
  236.9 1.9 copy-start.1
  236.9 491.3 %reduce-scatter.2.cloned.1.call-start = ((), (), s32[]{:S(2)}) async-start(), calls=%async_computation.3 | async-start | bytes 25165824 | tf_op jit(solution)/shard_map/reduce_scatter | solution.py:47
Sparse Core Ops, SparseCore 0:
  237.0 427.0 all-reduce.3
  704.3 23.8 reduce-scatter.1
where the time goes:
time: 749 us; the launch traced here: 748 us
  waiting for transfers between devices  398 us (53%)
  blocking collectives  203 us (27%)
  matrix products  61.2 us (8%)
  local copies, waits for them, and re-layouts  61 us (8%)
  between operations  13.5 us (2%)
  other arithmetic  11.3 us (2%)
    psum x1, waiting for transfers between devices, shards(): summed = lax.psum(partial_gram, 'rep')  374 us
    all_to_all x1, blocking collectives, shards(): lax.all_to_all(outgoing, 'expert', split_axis=0, concat_axis=2, tiled=True)  144 us
    psum x1, blocking collectives, shards(): lax.psum((jnp.sum(member, axis=0) * leader, jnp.sum(member * row_squares[...  44.5 us
    dot_general x1, matrix products, shards(): jnp.einsum('edf,edr->fer', up_weight, sketch, preferred_element_type=jnp....  40 us
    unnamed x12, local copies, waits for them, and re-layouts  24.1 us
    reduce_scatter x1, waiting for transfers between devices, shards(): lax.psum_scatter(jnp.einsum('edf,edr->fer', up_weight, sketch, preferred_...  24 us
  transfers between devices with their start and end apart: 2, of which 2 were waited for; matrix products, arithmetic and copies ran while one was open for 1% of the time, Pallas kernels for 0%

commit v1 on v0

--- a/solution.py
+++ b/solution.py
@@ -36,7 +36,10 @@
     summed_rows = lax.psum(partial_value, "hid")
     masked = summed_rows.astype(jnp.bfloat16)
     partial_gram = jnp.einsum("kmd,kmr->kdr", rows_here, masked, preferred_element_type=jnp.float32)
-    summed = lax.psum(partial_gram, "rep")
+    size, summed = (lax.axis_size("rep"), partial_gram)
+    for far in [1 << k for k in range(size.bit_length() - 1)]:
+        swap = [(i, i ^ far) for i in range(size)]
+        summed = summed + lax.ppermute(summed, "rep", swap)
     first_expert = lax.axis_index("expert") * exp_local
     row_counts = lax.dynamic_slice_in_dim(counts, first_expert, exp_local)
     square_sums = lax.dynamic_slice_in_dim(squares, first_expert, exp_local)

time: 749 us -> 1170 us (1.56)
  blocking collectives: 203 us -> 719 us
  waiting for transfers between devices: 398 us -> 295 us
    psum x1, blocking collectives: 44.5 us -> 560 us  [shards(): lax.psum((jnp.sum(member, axis=0) * leader, jnp.sum(member * row_squares[...]
    psum x1 -> x0, waiting for transfers between devices: 374 us -> none  [shards(): summed = lax.psum(partial_gram, 'rep')]
    ppermute x0 -> x2, waiting for transfers between devices: none -> 271 us  [shards(): summed = summed + lax.ppermute(summed, 'rep', swap)]
  transfers between devices with their start and end apart: 2 -> 3, of which waited for: 2 -> 2; matrix products, arithmetic and copies ran while one was open for 1% -> 1% of each run, Pallas kernels for 0% -> 0%
where the time goes in v1:
time: 1170 us
  blocking collectives  719 us (61%)
  waiting for transfers between devices  295 us (25%)
  local copies, waits for them, and re-layouts  59.4 us (5%)
  matrix products  58.4 us (5%)
  other arithmetic  17.4 us (1%)
  between operations  13.5 us (1%)
    psum x1, blocking collectives, shards(): lax.psum((jnp.sum(member, axis=0) * leader, jnp.sum(member * row_squares[...  560 us
    ppermute x2, waiting for transfers between devices, shards(): summed = summed + lax.ppermute(summed, 'rep', swap)  271 us
    all_to_all x1, blocking collectives, shards(): lax.all_to_all(outgoing, 'expert', split_axis=0, concat_axis=2, tiled=True)  144 us
    dot_general x1, matrix products, shards(): jnp.einsum('edf,edr->fer', up_weight, sketch, preferred_element_type=jnp....  40.2 us
    reduce_scatter x1, waiting for transfers between devices, shards(): lax.psum_scatter(jnp.einsum('edf,edr->fer', up_weight, sketch, preferred_...  24.5 us
  transfers between devices with their start and end apart: 3, of which 2 were waited for; matrix products, arithmetic and copies ran while one was open for 1% of the time, Pallas kernels for 0%

profile of v1, /device:TPU:0, one launch (start us, length us, event | category | flops | bytes accessed | tf_op | source)
XLA Modules:
  0.0 1167.8 jit_solution(6825678740568247530)
XLA Ops:
  6.5 0.8 copy.15
  7.9 2.3 reduce-window.6
  10.2 0.3 slice_reduce_fusion
  10.7 0.8 and_reduce_fusion
  11.5 0.7 multiply_reduce_fusion.2
  12.2 7.0 broadcast_in_dim.5
  19.3 13.6 %reshape.84 = bf16[1024,3072]{1,0:T(8,128)(2,1)} reshape(bf16[512,2,3072]{2,1,0:T(2,128)(2,1)} %broadcast_in_dim.5) | data formatting | bytes 12582912 | tf_op jit(solution)/shard_map/reshape | solution.py:28
  32.9 17.2 %scatter_custom_fusion = bf16[2048,3072]{1,0:T(8,128)(2,1)} fusion(s32[1024]{0:T(1024)S(1)} %broadcast_select_fusion, bf16[1024,3072]{1,0:T(8,128)(2,1)} %reshape.84, bf16[]{:T(256)} %constant.10.clone.1), kind=kCustom, calls=%fused_computation.3 | custom fusion | bytes 12583424
  50.0 144.0 %all_to_all.15 = bf16[4,2,256,3072]{3,2,1,0:T(8,128)(2,1)S(1)} all-to-all(bf16[4,2,256,3072]{3,2,1,0:T(8,128)(2,1)} %bitcast.35), channel_id=1, replica_groups=mesh['expert'=4,'rep'=4,'hid'=2] {'expert'}, dimensions={0} | all-to-all | bytes 25165824 | tf_op jit(solution)/shard_map/all_to_all | solution.py:32
  194.0 2.3 copy.18
  196.3 4.6 copy-done
  200.9 8.8 fusion.5
  209.7 14.9 %all-reduce.2 = bf16[2,1024,512]{2,1,0:T(8,128)(2,1)S(1)} all-reduce(f32[2,1024,512]{2,1,0:T(8,128)} %fusion.5), channel_id=1, replica_groups=mesh['expert'=4,'rep'=4,'hid'=2] {'hid'}, use_global_device_ids=true, to_apply=%region_4.0 | all-reduce | flops 1048576 | bytes 6291456 | tf_op jit(solution)/shard_map/psum | solution.py:36
  224.6 9.4 fusion.14
  234.0 1.8 collective-permute-start
  235.8 270.9 %collective-permute-done = f32[2,3072,512]{2,1,0:T(8,128)S(1)} collective-permute-done((f32[2,3072,512]{2,1,0:T(8,128)S(1)}, f32[2,3072,512]{2,1,0:T(8,128)S(1)}, u32[]{:S(2)}, u32[]{:S(2)}) %collective-permute-start) | collective-permute-done | bytes 12582944 | tf_op jit(solution)/shard_map/ppermute | solution.py:42
  506.7 6.1 add.51
  512.8 2.8 collective-permute-start.1
  515.6 0.7 multiply_reduce_fusion
  516.5 560.3 %all-reduce = (f32[8]{0:T(128)S(1)}, f32[8]{0:T(128)S(1)}) all-reduce(f32[8]{0:T(128)S(1)} %broadcast_multiply_fusion, f32[8]{0:T(128)S(1)} %multiply_reduce_fusion.1), channel_id=1, replica_groups=mesh['expert'=4,'rep'=4,'hid'=2] {'expert','rep','hid'}, use_global_device_ids=true, to_apply=%region_6.0 | all-reduce | flops 16 | bytes 128 | tf_op jit(solution)/shard_map/psum | solution.py:20
  1076.8 6.3 convert_element_type.35
  1083.1 40.2 %convolution_bitcast_fusion = f32[4096,2,512]{0,2,1:T(8,128)} fusion(bf16[2,3072,4096]{2,1,0:T(8,128)(2,1)} %param.7, f32[2,3072,512]{2,1,0:T(8,128)} %add.51, f32[2,3072,512]{2,1,0:T(8,128)} %collective-permute-done.1, f32[3072,512]{1,0:T(8,128)} %convert_element_type.35, f32[2]{0:T(128)S(1)} %get-tuple-element.9, f32[2]{0:T(128)S(1)} %get-tuple-element.10), kind=kOutput, calls=%fused_computation.2 | convolution fusion | flops 25785532416 | bytes 98566160 | tf_op jit(solution)/shard_map/edf,edr->fer/dot_general | solution.py:51
  1123.4 24.5 %reduce-scatter.2.cloned.1.call-done = f32[2048,2,512]{0,2,1:T(8,128)} async-done(((f32[4096,2,512]{0,2,1:T(8,128)}), f32[2048,2,512]{0,2,1:T(8,128)}) %reduce-scatter.2.cloned.1.call-update) | async-done | bytes 8388624 | tf_op jit(solution)/shard_map/reduce_scatter | solution.py:50
  1147.8 13.1 %copy.21 = f32[2048,2,512]{2,1,0:T(2,128)} copy(f32[2048,2,512]{0,2,1:T(8,128)} %reduce-scatter.2.cloned.1.call-done) | data formatting | bytes 16777216 | tf_op jit(solution)/shard_map/reduce_scatter | solution.py:50
  (26 shorter events, 1.2 us)
Async XLA Ops:
  6.5 1141.3 %reduce-scatter.2.cloned.1.call-start = ((), (), s32[]{:S(2)}) async-start(), calls=%async_computation.2 | async-start | bytes 25165824 | tf_op jit(solution)/shard_map/reduce_scatter | solution.py:50
  50.0 150.8 %slice-start = ((s8[6291456]{0:T(1024)(128)(4,1)}), s8[4194304]{0:T(1024)(128)(4,1)S(1)}, s32[]{:S(2)}) async-start(s8[6291456]{0:T(1024)(128)(4,1)} %bitcast.39), calls=%async_computation.3 | async-start | bytes 8388608
  194.0 6.9 slice-start.1
  196.3 4.6 copy-start
  234.0 281.5 %copy-start.2 = (s32[512,2]{0,1:T(2,128)S(1)}, s32[512,2]{0,1:T(2,128)}, u32[]{:S(2)}) copy-start(s32[512,2]{0,1:T(2,128)} %param.5) | copy-start | bytes 12292
  234.0 281.7 %copy-start.1 = (bf16[512,3072]{1,0:T(8,128)(2,1)S(1)}, bf16[512,3072]{1,0:T(8,128)(2,1)}, u32[]{:S(2)}) copy-start(bf16[512,3072]{1,0:T(8,128)(2,1)} %param.4) | copy-start | bytes 9437188
  234.0 272.7 %collective-permute-start = (f32[2,3072,512]{2,1,0:T(8,128)S(1)}, f32[2,3072,512]{2,1,0:T(8,128)S(1)}, u32[]{:S(2)}, u32[]{:S(2)}) collective-permute-start(f32[2,3072,512]{2,1,0:T(8,128)S(1)} %fusion.14), channel_id=1, source_target_pairs={{0,2},{2,0},{4,6},{6,4},{1,3},{3,1},{5,7},{7,5},{8,10},{10,8},{12,... | collective-permute-start | bytes 37748744 | tf_op jit(solution)/shard_map/ppermute | solution.py:42
  512.8 570.4 %collective-permute-start.1 = (f32[2,3072,512]{2,1,0:T(8,128)}, f32[2,3072,512]{2,1,0:T(8,128)}, u32[]{:S(2)}, u32[]{:S(2)}) collective-permute-start(f32[2,3072,512]{2,1,0:T(8,128)} %add.51), channel_id=1, source_target_pairs={{0,4},{2,6},{4,0},{6,2},{1,5},{3,7},{5,1},{7,3},{8,12},{10,14},{12... | collective-permute-start | bytes 37748744 | tf_op jit(solution)/shard_map/ppermute | solution.py:42
Sparse Core Ops, SparseCore 0:
  1123.5 24.2 reduce-scatter.1
